TPU v7x, 32 devices: a whole 2x2x4 slice. The times are simulated.
32 devices in a mesh: seq: 8 (over z, y), head: 4 (over x, core).
Axes of the slice: x: 2, y: 2, z: 4, core: 2. Of those that a mesh axis runs over, the one named last changes fastest.
Arguments:
- queries: bfloat16 [2048, 2048], P(('seq', 'head')), may hold values from -200 to 200
- keys: bfloat16 [2048, 2048], P(('seq', 'head')), may hold values from -15 to 15
- values: bfloat16 [2048, 2048], P(('seq', 'head')), may hold values from -6 to 6
- random_blocks: int32 [32, 16, 3], P('seq', 'head'), may hold values from 0 to 31, as said below
- global_blocks: int32 [2], replicated, may hold values from 0 to 31, as said below
Outputs:
- attention: float32 [2048, 2048], P('seq', 'head')
Inputs may be any that keep to these rules, and one draw needn't show every extreme that they name: `random_blocks`: over the 4 query blocks and 4 heads of one device (one index of seq and one of head), at most 9 entries name blocks of any one shard of 4 consecutive blocks; in every draw some device names exactly 9 blocks of one shard. Entries may repeat and may fall on the window or on a global block. `global_blocks`: two different block numbers; one of them is 31.
All inputs are finite; a program needn't handle non-finite values.
Results may differ from a plain program's by a relative error of at most 0.0023.
Values may be sent and summed in bfloat16 or wider, within the bound.
A program may use at most 128 MiB of HBM per device.

v0:
```python
import math

import jax
import jax.numpy as jnp
from jax import lax
from jax.sharding import PartitionSpec as P

HEAD_DIM = 128
BLK = 64


MASKED = -1e30


def extended(block, sides, width):
    for axis, dim in sides:
        count = lax.axis_size(axis)
        forward = [(i, i + 1) for i in range(count - 1)]
        backward = [(target, source) for source, target in forward]
        low = lax.ppermute(
            lax.slice_in_dim(block, block.shape[dim] - width, None, axis=dim), axis, forward
        )
        high = lax.ppermute(lax.slice_in_dim(block, 0, width, axis=dim), axis, backward)
        block = jnp.concatenate([low, block, high], axis=dim)
    return block


def combined_all(value, axis, join):
    pieces = jax.tree.map(lambda part: lax.all_gather(part, axis), value)
    head = jax.tree.map(lambda part: part[0], pieces)
    tail = jax.tree.map(lambda part: part[1:], pieces)
    so_far, _ = lax.scan(lambda so_far, slab: (join(so_far, slab), None), head, tail)
    return so_far


def merge_parts(former, latter):
    peaks = jnp.maximum(former[0], latter[0])
    former_fade = jnp.exp(former[0] - peaks)
    latter_fade = jnp.exp(latter[0] - peaks)
    return (
        peaks,
        former[1] * former_fade + latter[1] * latter_fade,
        former[2] * former_fade[..., None] + latter[2] * latter_fade[..., None],
    )


def soft_parts(scores):
    peaks = jnp.max(scores, axis=(-2, -1))
    powers = jnp.exp(scores - peaks[..., None, None])
    return (peaks, jnp.sum(powers, axis=(-2, -1)), powers.astype(jnp.bfloat16))


def make_requests(rand_lists, seq_count, capacity):
    blk_dev, heads_dev, rand_count = rand_lists.shape
    flat_list = rand_lists.reshape(-1)
    owners = flat_list // blk_dev
    head_ids = jnp.broadcast_to(
        jnp.arange(heads_dev, dtype=jnp.int32)[None, :, None], rand_lists.shape
    ).reshape(-1)
    item_ids = flat_list % blk_dev * heads_dev + head_ids
    position = jnp.arange(flat_list.shape[0], dtype=jnp.int32)
    earlier = (owners[:, None] == owners[None, :]) & (position[None, :] < position[:, None])
    slot_ids = owners * capacity + jnp.sum(earlier.astype(jnp.int32), axis=1)
    requests = jnp.zeros((seq_count * capacity,), jnp.int32).at[slot_ids].set(item_ids)
    sources = jnp.zeros((seq_count * capacity,), jnp.int32).at[slot_ids].set(position)
    return (requests.reshape(seq_count, capacity), slot_ids, sources)


def shards(queries, keys, values, random_blocks, global_blocks):
    seq_count = lax.axis_size("seq")
    seq_index = lax.axis_index("seq")
    query_rows, key_rows, value_rows = (
        lax.all_to_all(queries, "head", split_axis=1, concat_axis=0, tiled=True),
        lax.all_to_all(keys, "head", split_axis=1, concat_axis=0, tiled=True),
        lax.all_to_all(values, "head", split_axis=1, concat_axis=0, tiled=True),
    )
    tokens = query_rows.shape[0]
    blk_dev = tokens // BLK
    heads_dev = query_rows.shape[1] // HEAD_DIM
    rand_count = random_blocks.shape[2]
    glob_count = global_blocks.shape[0]
    total_blocks = blk_dev * seq_count
    first_block = seq_index * blk_dev
    capacity = (blk_dev * heads_dev * rand_count * 3 // 2 + seq_count - 1) // seq_count
    score_scale = 1.0 / math.sqrt(HEAD_DIM)
    shape_four = (blk_dev, BLK, heads_dev, HEAD_DIM)
    query_four = query_rows.reshape(shape_four)
    key_four = key_rows.reshape(shape_four)
    value_four = value_rows.reshape(shape_four)
    paired = jnp.stack([key_rows, value_rows])
    padded = extended(paired, (("seq", 1),), BLK)
    padded = padded.reshape(2, blk_dev + 2, BLK, heads_dev, HEAD_DIM)
    window = jnp.stack([padded[:, offset : offset + blk_dev] for offset in range(3)], axis=2)
    near_ids = (
        first_block
        + jnp.arange(blk_dev, dtype=jnp.int32)[:, None]
        + jnp.arange(-1, 2, dtype=jnp.int32)[None, :]
    )
    inside = (near_ids >= 0) & (near_ids < total_blocks)
    stacked = jnp.stack([query_rows, key_rows, value_rows]).reshape(
        3, blk_dev, BLK, heads_dev * HEAD_DIM
    )
    owned_mask = global_blocks // blk_dev == seq_index
    local_ids = jnp.where(owned_mask, global_blocks - first_block, 0)
    picked = (
        jnp.take(stacked, local_ids, axis=1).astype(jnp.float32)
        * owned_mask.astype(jnp.float32)[None, :, None, None]
    )
    glob_rows = lax.psum(picked, "seq").astype(jnp.bfloat16)
    glob_rows = glob_rows.reshape(3, glob_count, BLK, heads_dev, HEAD_DIM)
    requests, slot_ids, sources = make_requests(random_blocks, seq_count, capacity)
    incoming = lax.all_to_all(requests, "seq", split_axis=0, concat_axis=0, tiled=True)

    def by_block(row_data):
        return (
            row_data.reshape(shape_four)
            .transpose(0, 2, 1, 3)
            .reshape(blk_dev * heads_dev, BLK, HEAD_DIM)
        )

    pair_blocks = jnp.stack([by_block(key_rows), by_block(value_rows)], axis=1)
    served = pair_blocks[incoming]
    key_win, value_win = (window[0], window[1])
    win_scores = (
        jnp.einsum("jqhd,jwkhd->jhqwk", query_four, key_win, preferred_element_type=jnp.float32)
        * score_scale
    )
    win_scores = jnp.where(inside[:, None, None, :, None], win_scores, MASKED)
    glob_scores = (
        jnp.einsum("jqhd,gkhd->jhqgk", query_four, glob_rows[1], preferred_element_type=jnp.float32)
        * score_scale
    )
    split_at = 3 + glob_count
    arrived_pairs = lax.all_to_all(served, "seq", split_axis=0, concat_axis=0, tiled=True)
    tail = arrived_pairs.shape[2:]
    rand_pairs = arrived_pairs.reshape((seq_count * capacity,) + tail)[slot_ids].reshape(
        (blk_dev, heads_dev, rand_count) + tail
    )
    rand_scores = (
        jnp.einsum(
            "jqhd,jhrkd->jhqrk",
            query_four,
            rand_pairs[:, :, :, 0],
            preferred_element_type=jnp.float32,
        )
        * score_scale
    )
    peaks, totals, weights = soft_parts(
        jnp.concatenate([win_scores, glob_scores, rand_scores], axis=3)
    )
    sums_all = jnp.einsum(
        "jhqwk,jwkhd->jhqd", weights[:, :, :, 0:3], value_win, preferred_element_type=jnp.float32
    )
    sums_all = sums_all + jnp.einsum(
        "jhqgk,gkhd->jhqd",
        weights[:, :, :, 3:split_at],
        glob_rows[2],
        preferred_element_type=jnp.float32,
    )
    sums_all = sums_all + jnp.einsum(
        "jhqrk,jhrkd->jhqd",
        weights[:, :, :, split_at:],
        rand_pairs[:, :, :, 1],
        preferred_element_type=jnp.float32,
    )
    running = (peaks, totals, sums_all)
    sparse_out = (running[2] / running[1][..., None]).transpose(0, 2, 1, 3)
    full_scores = (
        jnp.einsum("gqhd,jkhd->hgqjk", glob_rows[0], key_four, preferred_element_type=jnp.float32)
        * score_scale
    )
    full_peaks, full_totals, full_weights = soft_parts(full_scores)
    full_sum = jnp.einsum(
        "hgqjk,jkhd->hgqd", full_weights, value_four, preferred_element_type=jnp.float32
    )
    merged = combined_all((full_peaks, full_totals, full_sum), "seq", merge_parts)
    glob_out = (merged[2] / merged[1][..., None]).transpose(1, 2, 0, 3)
    block_ids = first_block + jnp.arange(blk_dev, dtype=jnp.int32)
    result = sparse_out
    for glob_id in range(glob_count):
        matches = (block_ids == global_blocks[glob_id])[:, None, None, None]
        result = jnp.where(matches, glob_out[glob_id][None], result)
    return result.reshape(tokens, heads_dev * HEAD_DIM)


def solution(mesh):
    in_specs = (
        P(("seq", "head"), None),
        P(("seq", "head"), None),
        P(("seq", "head"), None),
        P("seq", "head", None),
        P(),
    )
    out_specs = P("seq", "head")
    return jax.shard_map(shards, mesh=mesh, in_specs=in_specs, out_specs=out_specs, check_vma=False)
```

profile of v0, /device:TPU:0, one launch (start us, length us, event | category | flops | bytes accessed | tf_op | source)
XLA Modules:
  0.0 225.2 jit_solution(5430043411792527505)
XLA Ops:
  6.5 1.7 copy.232
  8.3 4.2 %all-to-all-start.1 = ((bf16[64,4,512]{2,0,1:T(8,128)(2,1)}), bf16[64,4,512]{2,0,1:T(8,128)(2,1)S(1)}, u32[]{:S(2)}, u32[]{:S(2)}) async-start(bf16[64,4,512]{2,0,1:T(8,128)(2,1)} %bitcast.155), calls=%async_computation.1 | async-start | bytes 524288 | tf_op jit(solution)/shard_map/all_to_all | solution.py:74
  12.5 1.7 copy.231
  14.2 4.3 %all-to-all-done.1 = bf16[64,4,512]{2,0,1:T(8,128)(2,1)S(1)} async-done(((bf16[64,4,512]{2,0,1:T(8,128)(2,1)}), bf16[64,4,512]{2,0,1:T(8,128)(2,1)S(1)}, u32[]{:S(2)}, u32[]{:S(2)}) %all-to-all-start.1) | async-done | bytes 262176 | tf_op jit(solution)/shard_map/all_to_all | solution.py:74
  18.5 3.4 %all-to-all-start.2 = ((bf16[64,4,512]{2,0,1:T(8,128)(2,1)}), bf16[64,4,512]{2,0,1:T(8,128)(2,1)S(1)}, u32[]{:S(2)}, u32[]{:S(2)}) async-start(bf16[64,4,512]{2,0,1:T(8,128)(2,1)} %bitcast.154), calls=%async_computation.2 | async-start | bytes 524288 | tf_op jit(solution)/shard_map/all_to_all | solution.py:75
  22.0 0.7 copy.233
  22.7 5.2 %all-to-all-done.2 = bf16[64,4,512]{2,0,1:T(8,128)(2,1)S(1)} async-done(((bf16[64,4,512]{2,0,1:T(8,128)(2,1)}), bf16[64,4,512]{2,0,1:T(8,128)(2,1)S(1)}, u32[]{:S(2)}, u32[]{:S(2)}) %all-to-all-start.2) | async-done | bytes 262176 | tf_op jit(solution)/shard_map/all_to_all | solution.py:75
  27.9 3.4 %all-to-all-start = ((bf16[64,4,512]{2,0,1:T(8,128)(2,1)}), bf16[64,4,512]{2,0,1:T(8,128)(2,1)S(1)}, u32[]{:S(2)}, u32[]{:S(2)}) async-start(bf16[64,4,512]{2,0,1:T(8,128)(2,1)} %bitcast.156), calls=%async_computation | async-start | bytes 524288 | tf_op jit(solution)/shard_map/all_to_all | solution.py:73
  31.4 5.9 %all-to-all-done = bf16[64,4,512]{2,0,1:T(8,128)(2,1)S(1)} async-done(((bf16[64,4,512]{2,0,1:T(8,128)(2,1)}), bf16[64,4,512]{2,0,1:T(8,128)(2,1)S(1)}, u32[]{:S(2)}, u32[]{:S(2)}) %all-to-all-start) | async-done | bytes 262176 | tf_op jit(solution)/shard_map/all_to_all | solution.py:73
  38.1 46.4 %all-reduce.1 = bf16[3,2,64,512]{3,2,0,1:T(8,128)(2,1)S(1)} all-reduce(f32[3,2,64,512]{3,2,0,1:T(8,128)S(1)} %multiply_bitcast_fusion.1), channel_id=1, replica_groups=mesh['seq'=8,'head'=4] {'seq'}, use_global_device_ids=true, to_apply=%region_0.1 | all-reduce | flops 196608 | bytes 1179648 | tf_op jit(solution)/shard_map/psum | solution.py:109
  85.1 1.0 convolution_bitcast_fusion.3
  86.8 0.7 scatter_custom_fusion
  88.2 3.3 %all-to-all-start.3 = ((s32[8,1,9]{2,1,0:T(1,128)}), s32[8,1,9]{2,1,0:T(1,128)S(1)}, u32[]{:S(2)}, u32[]{:S(2)}) async-start(s32[8,1,9]{2,1,0:T(1,128)} %bitcast.40), calls=%async_computation.3 | async-start | bytes 8192 | tf_op jit(solution)/shard_map/all_to_all | solution.py:112
  92.8 1.8 broadcast_compare_fusion
  94.7 3.2 %all-to-all-done.3 = s32[8,1,9]{2,1,0:T(1,128)S(1)} async-done(((s32[8,1,9]{2,1,0:T(1,128)}), s32[8,1,9]{2,1,0:T(1,128)S(1)}, u32[]{:S(2)}, u32[]{:S(2)}) %all-to-all-start.3) | async-done | bytes 320 | tf_op jit(solution)/shard_map/all_to_all | solution.py:112
  98.2 31.1 %all-gather.1 = f32[32,2,64]{2,1,0:T(2,128)S(1)} all-gather(f32[4,2,64]{2,1,0:T(2,128)S(1)} %fusion.13), channel_id=3, replica_groups=mesh['seq'=8,'head'=4] {'seq'}, dimensions={0}, use_global_device_ids=true | all-gather | bytes 18432 | tf_op jit(solution)/shard_map/all_gather | solution.py:29
  129.9 30.7 %all-gather = f32[32,2,64]{2,1,0:T(2,128)S(1)} all-gather(f32[4,2,64]{2,1,0:T(2,128)S(1)} %get-tuple-element.88), channel_id=2, replica_groups=mesh['seq'=8,'head'=4] {'seq'}, dimensions={0}, use_global_device_ids=true | all-gather | bytes 18432 | tf_op jit(solution)/shard_map/all_gather | solution.py:29
  161.9 2.6 %collective-permute-start = (bf16[2,64,512]{2,1,0:T(8,128)(2,1)}, bf16[2,64,512]{2,1,0:T(8,128)(2,1)}, u32[]{:S(2)}, u32[]{:S(2)}) collective-permute-start(bf16[2,64,512]{2,1,0:T(8,128)(2,1)} %get-tuple-element.71), channel_id=1, source_target_pairs={{0,4},{4,8},{8,12},{12,16},{16,20},{20,24},{24,28},{1,5},{5,9},{9,... | collective-permute-start | bytes 393224 | tf_op jit(solution)/shard_map/ppermute | solution.py:20
  164.5 1.3 collective-permute-start.1
  165.9 0.7 squeeze.54
  166.8 2.5 %gather_fusion.1 = bf16[72,2,64,128]{3,2,1,0:T(8,128)(2,1)} fusion(bf16[16,2,64,128]{3,2,0,1:T(8,128)(2,1)S(1)} %pad_maximum_fusion.3, s32[1024]{0:T(1024)S(1)} %pad_clamp_fusion.1), kind=kCustom, calls=%fused_computation.1 | custom fusion | bytes 4718880 | tf_op jit(solution)/shard_map/gather | solution.py:122
  169.2 5.5 %all-to-all-start.4 = ((bf16[8,9,2,64,128]{4,3,2,1,0:T(8,128)(2,1)}), bf16[8,9,2,64,128]{4,3,2,1,0:T(8,128)(2,1)S(1)}, u32[]{:S(2)}, u32[]{:S(2)}) async-start(bf16[8,9,2,64,128]{4,3,2,1,0:T(8,128)(2,1)} %bitcast.42), calls=%async_computation.4 | async-start | bytes 4718592 | tf_op jit(solution)/shard_map/all_to_all | solution.py:134
  174.7 1.3 fusion.40
  176.1 2.6 %copy.145 = f32[4,4,64,2,64]{2,4,3,1,0:T(8,128)} copy(f32[4,4,64,2,64]{4,2,0,3,1:T(8,128)} %get-tuple-element.87) | data formatting | bytes 1048576 | tf_op jit(solution)/shard_map/mul | solution.py:130
  179.3 1.9 pad_maximum_fusion.2
  181.3 1.7 reshape.285
  184.3 1.1 copy-done.3
  185.5 1.6 fusion.39
  187.1 3.0 %slice.121 = f32[28,2,64,128]{3,2,1,0:T(8,128)} slice(f32[32,2,64,128]{3,2,1,0:T(8,128)} %all-gather.5.cloned.1.call-done), slice={[4:32], [0:2], [0:64], [0:128]} | slice | bytes 3670016 | tf_op jit(solution)/shard_map/slice | solution.py:31
  190.2 13.6 %while.14 = (s32[]{:T(128)}, f32[4,2,64]{2,1,0:T(2,128)S(1)}, f32[4,2,64]{2,1,0:T(2,128)S(1)}, f32[4,2,64,128]{3,2,1,0:T(8,128)S(1)}, f32[7,4,2,64]{3,2,1,0:T(2,...) while((s32[]{:T(128)}, f32[4,2,64]{2,1,0:T(2,128)S(1)}, ...), condition=%wide.region_4.5_spmd, body=%wide.region_3.4_spmd.sunk | while | flops 199682 | bytes 807005 | solution.py:32
  190.2 0.7 fusion.46
  190.9 1.2 fusion.47
  192.9 1.2 fusion.47
  194.1 0.7 fusion.46
  194.8 1.2 fusion.47
  196.0 0.7 fusion.46
  196.8 1.2 fusion.47
  198.0 0.7 fusion.46
  198.7 1.2 fusion.47
  200.0 0.7 fusion.46
  200.7 1.2 fusion.47
  202.6 1.2 fusion.47
  204.0 4.8 %all-to-all-done.4 = bf16[8,9,2,64,128]{4,3,2,1,0:T(8,128)(2,1)S(1)} async-done(((bf16[8,9,2,64,128]{4,3,2,1,0:T(8,128)(2,1)}), bf16[8,9,2,64,128]{4,3,2,1,0:T(8,128)(2,1)S(1)}, u32[]{:S(2)}, u32[]{:S(2)}) %all-to-all-start.4) | async-done | bytes 2359328 | tf_op jit(solution)/shard_map/all_to_all | solution.py:134
  208.8 2.0 gather_fusion.2
  210.8 1.5 copy.143
  212.7 0.8 copy-done.2
  214.0 1.0 fusion.4
  217.5 0.8 copy.229
  (94 shorter events, 13.4 us)
Async XLA Ops:
  6.5 15.4 %copy-start.14 = (s32[2]{0:T(128)S(1)}, s32[2]{0:T(128)}, u32[]{:S(2)}) copy-start(s32[2]{0:T(128)} %param.11) | copy-start | bytes 28
  6.5 15.4 %copy-start.9 = (bf16[64,2048]{1,0:T(8,128)(2,1)S(1)}, bf16[64,2048]{1,0:T(8,128)(2,1)}, u32[]{:S(2)}) copy-start(bf16[64,2048]{1,0:T(8,128)(2,1)} %param.7) | copy-start | bytes 786436
  8.3 10.2 %all-to-all-start.1 = ((bf16[64,4,512]{2,0,1:T(8,128)(2,1)}), bf16[64,4,512]{2,0,1:T(8,128)(2,1)S(1)}, u32[]{:S(2)}, u32[]{:S(2)}) async-start(bf16[64,4,512]{2,0,1:T(8,128)(2,1)} %bitcast.155), calls=%async_computation.1 | async-start | bytes 524288 | tf_op jit(solution)/shard_map/all_to_all | solution.py:74
  18.5 9.4 %all-to-all-start.2 = ((bf16[64,4,512]{2,0,1:T(8,128)(2,1)}), bf16[64,4,512]{2,0,1:T(8,128)(2,1)S(1)}, u32[]{:S(2)}, u32[]{:S(2)}) async-start(bf16[64,4,512]{2,0,1:T(8,128)(2,1)} %bitcast.154), calls=%async_computation.2 | async-start | bytes 524288 | tf_op jit(solution)/shard_map/all_to_all | solution.py:75
  27.9 133.3 %copy-start = (bf16[64,4,512]{2,0,1:T(8,128)(2,1)}, bf16[64,4,512]{2,0,1:T(8,128)(2,1)S(1)}, u32[]{:S(2)}) copy-start(bf16[64,4,512]{2,0,1:T(8,128)(2,1)S(1)} %all-to-all-done.2) | copy-start | bytes 786436
  27.9 9.4 %all-to-all-start = ((bf16[64,4,512]{2,0,1:T(8,128)(2,1)}), bf16[64,4,512]{2,0,1:T(8,128)(2,1)S(1)}, u32[]{:S(2)}, u32[]{:S(2)}) async-start(bf16[64,4,512]{2,0,1:T(8,128)(2,1)} %bitcast.156), calls=%async_computation | async-start | bytes 524288 | tf_op jit(solution)/shard_map/all_to_all | solution.py:73
  31.3 155.8 %all-gather.5.cloned.1.call-start = ((), (), s32[]{:S(2)}) async-start(), calls=%async_computation.5 | async-start | bytes 2359296 | tf_op jit(solution)/shard_map/all_gather | solution.py:29
  84.8 1.4 copy-start.13
  88.2 9.7 %all-to-all-start.3 = ((s32[8,1,9]{2,1,0:T(1,128)}), s32[8,1,9]{2,1,0:T(1,128)S(1)}, u32[]{:S(2)}, u32[]{:S(2)}) async-start(s32[8,1,9]{2,1,0:T(1,128)} %bitcast.40), calls=%async_computation.3 | async-start | bytes 8192 | tf_op jit(solution)/shard_map/all_to_all | solution.py:112
  129.3 40.0 %copy-start.10 = (f32[32,2,64]{2,1,0:T(2,128)}, f32[32,2,64]{2,1,0:T(2,128)S(1)}, u32[]{:S(2)}) copy-start(f32[32,2,64]{2,1,0:T(2,128)S(1)} %all-gather.1) | copy-start | bytes 49156
  160.6 8.7 %copy-start.11 = (f32[32,2,64]{2,1,0:T(2,128)}, f32[32,2,64]{2,1,0:T(2,128)S(1)}, u32[]{:S(2)}) copy-start(f32[32,2,64]{2,1,0:T(2,128)S(1)} %all-gather) | copy-start | bytes 49156
  161.9 17.4 %collective-permute-start = (bf16[2,64,512]{2,1,0:T(8,128)(2,1)}, bf16[2,64,512]{2,1,0:T(8,128)(2,1)}, u32[]{:S(2)}, u32[]{:S(2)}) collective-permute-start(bf16[2,64,512]{2,1,0:T(8,128)(2,1)} %get-tuple-element.71), channel_id=1, source_target_pairs={{0,4},{4,8},{8,12},{12,16},{16,20},{20,24},{24,28},{1,5},{5,9},{9,... | collective-permute-start | bytes 393224 | tf_op jit(solution)/shard_map/ppermute | solution.py:20
  164.5 14.8 %collective-permute-start.1 = (bf16[2,64,512]{2,1,0:T(8,128)(2,1)}, bf16[2,64,512]{2,1,0:T(8,128)(2,1)}, u32[]{:S(2)}, u32[]{:S(2)}) collective-permute-start(bf16[2,64,512]{2,1,0:T(8,128)(2,1)} %get-tuple-element.72), channel_id=1, source_target_pairs={{4,0},{8,4},{12,8},{16,12},{20,16},{24,20},{28,24},{5,1},{9,5},{13... | collective-permute-start | bytes 393224 | tf_op jit(solution)/shard_map/ppermute | solution.py:23
  165.9 8.9 %copy-start.5 = (bf16[4,64,4,128]{3,2,1,0:T(4,128)(2,1)}, bf16[4,64,4,128]{3,2,1,0:T(4,128)(2,1)S(1)}, u32[]{:S(2)}) copy-start(bf16[4,64,4,128]{3,2,1,0:T(4,128)(2,1)S(1)} %reshape.286) | copy-start | bytes 786436
  169.2 5.5 %copy-start.8 = (bf16[2,64,4,128]{3,2,1,0:T(4,128)(2,1)S(1)}, bf16[2,64,4,128]{3,2,1,0:T(4,128)(2,1)}, u32[]{:S(2)}) copy-start(bf16[2,64,4,128]{3,2,1,0:T(4,128)(2,1)} %squeeze.54) | copy-start | bytes 393220
  169.2 39.6 %all-to-all-start.4 = ((bf16[8,9,2,64,128]{4,3,2,1,0:T(8,128)(2,1)}), bf16[8,9,2,64,128]{4,3,2,1,0:T(8,128)(2,1)S(1)}, u32[]{:S(2)}, u32[]{:S(2)}) async-start(bf16[8,9,2,64,128]{4,3,2,1,0:T(8,128)(2,1)} %bitcast.42), calls=%async_computation.4 | async-start | bytes 4718592 | tf_op jit(solution)/shard_map/all_to_all | solution.py:134
  174.7 4.6 %copy-start.1 = (bf16[64,4,512]{2,0,1:T(8,128)(2,1)S(1)}, bf16[64,4,512]{2,0,1:T(8,128)(2,1)}, u32[]{:S(2)}) copy-start(bf16[64,4,512]{2,0,1:T(8,128)(2,1)} %copy-done) | copy-start | bytes 786436
  184.1 1.4 copy-start.6
  184.1 1.4 copy-start.16
  184.3 1.2 copy-start.3
  187.1 3.1 %slice-start.1 = ((f32[32,2,64]{2,1,0:T(2,128)}), f32[4,2,64]{2,1,0:T(2,128)S(1)}, s32[]{:S(2)}) async-start(f32[32,2,64]{2,1,0:T(2,128)} %copy-done.10), calls=%async_computation.7 | async-start | bytes 8192 | tf_op jit(solution)/shard_map/slice | solution.py:30
  187.1 3.1 %slice-start.2 = ((f32[32,2,64]{2,1,0:T(2,128)}), f32[4,2,64]{2,1,0:T(2,128)S(1)}, s32[]{:S(2)}) async-start(f32[32,2,64]{2,1,0:T(2,128)} %copy-done.11), calls=%async_computation.8 | async-start | bytes 8192 | tf_op jit(solution)/shard_map/slice | solution.py:30
  187.1 3.0 %slice-start = ((f32[32,2,64,128]{3,2,1,0:T(8,128)}), f32[4,2,64,128]{3,2,1,0:T(8,128)S(1)}, s32[]{:S(2)}) async-start(f32[32,2,64,128]{3,2,1,0:T(8,128)} %all-gather.5.cloned.1.call-done), calls=%async_computation.6 | async-start | bytes 524288 | tf_op jit(solution)/shard_map/slice | solution.py:30
  212.3 1.2 copy-start.2
  212.3 1.7 copy-start.7
  214.0 1.4 copy-start.4
  215.9 0.9 copy-start.12
  215.9 0.9 copy-start.15
Sparse Core Ops, SparseCore 0:
  86.3 48.8 all-gather.4
where the time goes:
time: 228 us; the launch traced here: 225 us
  blocking collectives  108 us (47%)
  local copies, waits for them, and re-layouts  29.2 us (13%)
  starting transfers between devices  23.7 us (10%)
  waiting for transfers between devices  23.4 us (10%)
  other arithmetic  20.7 us (9%)
  between operations  13.9 us (6%)
  matrix products  5.95 us (3%)
    all_gather x2, blocking collectives, combined_all(): pieces = jax.tree.map(lambda part: lax.all_gather(part, axis), value)  61.7 us
    psum x1, blocking collectives, shards(): glob_rows = lax.psum(picked, 'seq').astype(jnp.bfloat16)  46.4 us
    add x7, other arithmetic, merge_parts(): former[2] * former_fade[..., None] + latter[2] * latter_fade[..., None]  8.46 us
    all_to_all x1, waiting for transfers between devices, shards(): lax.all_to_all(queries, 'head', split_axis=1, concat_axis=0, tiled=True)  5.91 us
    all_to_all x1, starting transfers between devices, shards(): lax.all_to_all(served, 'seq', split_axis=0, concat_axis=0, tiled=True)  5.48 us
    all_to_all x1, waiting for transfers between devices, shards(): lax.all_to_all(values, 'head', split_axis=1, concat_axis=0, tiled=True)  5.2 us
    add x7, other arithmetic, merge_parts(): former[1] * former_fade + latter[1] * latter_fade  5.05 us
    all_to_all x1, waiting for transfers between devices, shards(): lax.all_to_all(served, 'seq', split_axis=0, concat_axis=0, tiled=True)  4.8 us
  transfers between devices with their start and end apart: 8, of which 5 were waited for; matrix products, arithmetic and copies ran while one was open for 18% of the time, Pallas kernels for 0%

commit v1 on v0

--- a/solution.py
+++ b/solution.py
@@ -1,8 +1,11 @@
+import functools
 import math
 
 import jax
 import jax.numpy as jnp
 from jax import lax
+from jax.experimental import pallas as pl
+from jax.experimental.pallas import tpu as pltpu
 from jax.sharding import PartitionSpec as P
 
 HEAD_DIM = 128
@@ -66,7 +69,7 @@
     return (requests.reshape(seq_count, capacity), slot_ids, sources)
 
 
-def shards(queries, keys, values, random_blocks, global_blocks):
+def exchanged(queries, keys, values, random_blocks, global_blocks):
     seq_count = lax.axis_size("seq")
     seq_index = lax.axis_index("seq")
     query_rows, key_rows, value_rows = (
@@ -183,6 +186,306 @@
     return result.reshape(tokens, heads_dev * HEAD_DIM)
 
 
+GATHER_LIMIT = 16 * 2**20
+
+
+def gathered_kernel(
+    seq_count, head_count, rand_count, glob_count,
+    q_hbm, k_hbm, v_hbm, rand_ref, glob_ref, out_ref,
+    pool, q_all, stage, q_stage, listed, peak_ref, total_ref, acc_ref,
+    local_sem, send_sem, recv_sem, q_send_sem, q_recv_sem,
+):
+    seq = lax.axis_index("seq")
+    head = lax.axis_index("head")
+    depth = seq_count // 2
+    z, y = seq // 2, seq % 2
+    rows, width = q_all.shape[1], q_all.shape[2]
+    heads_dev = width // HEAD_DIM
+    tokens = head_count * rows
+    classes = head_count
+
+    def lane(k):
+        return ((head // 2 + k // 2) % (head_count // 2)) * 2 + (head % 2 + k % 2) % 2
+
+    def shard(dz, dy):
+        return ((z + dz) % depth) * 2 + (y + dy) % 2
+
+    def spot(dz, dy, k):
+        return shard(dz, dy) * head_count + lane(k)
+
+    loads = []
+    for k in range(classes):
+        cols = pl.ds(pl.multiple_of(lane(k) * width, 128), width)
+        target = pool.at[spot(0, 0, 0)] if k == 0 else stage.at[k - 1]
+        q_target = q_all.at[head] if k == 0 else q_stage.at[k - 1]
+        trio = []
+        for n, (source, dest) in enumerate(
+            ((k_hbm, target.at[0]), (v_hbm, target.at[1]), (q_hbm, q_target))
+        ):
+            trio.append(pltpu.make_async_copy(source.at[:, cols], dest, local_sem.at[k * 3 + n]))
+        loads.append(trio)
+    for n in range(3):
+        for trio in loads if n == 2 else ():
+            trio[n].start()
+        for trio in loads if n == 0 else ():
+            trio[0].start()
+            trio[1].start()
+
+    barrier = pltpu.get_barrier_semaphore()
+    friends = [{"seq": seq, "head": lane(k)} for k in range(1, classes)]
+    friends.append({"seq": shard(0, 1), "head": head})
+    friends.append({"seq": shard(1, 0), "head": head})
+    friends.append({"seq": shard(-1, 0), "head": head})
+    for friend in friends:
+        pl.semaphore_signal(barrier, inc=1, device_id=friend, device_id_type=pl.DeviceIdType.MESH)
+
+    query_block = seq * (tokens // BLK) + lax.broadcasted_iota(jnp.int32, (1, tokens), 1) // BLK
+    local_block = lax.broadcasted_iota(jnp.int32, (1, tokens), 1) // BLK
+    for hd in range(heads_dev):
+        for r in range(rand_count):
+            names = jnp.zeros((1, tokens), jnp.int32)
+            for b in range(tokens // BLK):
+                names = jnp.where(local_block == b, rand_ref[b, hd, r], names)
+            listed[pl.ds(hd * rand_count + r, 1), :] = names
+    is_glob = query_block == glob_ref[0]
+    for g in range(1, glob_count):
+        is_glob = is_glob | (query_block == glob_ref[g])
+    glob_row = jnp.where(is_glob, 1, 0)
+    peak_ref[...] = jnp.full_like(peak_ref, MASKED)
+    total_ref[...] = jnp.zeros_like(total_ref)
+    acc_ref[...] = jnp.zeros_like(acc_ref)
+
+    for trio in loads:
+        trio[0].wait()
+        trio[1].wait()
+    for trio in loads:
+        trio[2].wait()
+    pl.semaphore_wait(barrier, len(friends))
+
+    pending = []
+    landed = {(0, 0, 0)}
+
+    def remote(source, dest, sender, receiver, device):
+        return pltpu.make_async_remote_copy(
+            src_ref=source, dst_ref=dest, send_sem=sender, recv_sem=receiver,
+            device_id=device, device_id_type=pl.DeviceIdType.MESH,
+        )
+
+    def push(dz, dy, k, device):
+        place = spot(dz, dy, k)
+        copy = remote(
+            pool.at[place], pool.at[place], send_sem.at[len(pending)], recv_sem.at[place], device
+        )
+        copy.start()
+        pending.append(copy)
+
+    up = {"seq": shard(1, 0), "head": head}
+    down = {"seq": shard(-1, 0), "head": head}
+    across = {"seq": shard(0, 1), "head": head}
+
+    def arrive(dz, dy, k):
+        key = (dz % depth, dy % 2, k)
+        if key in landed:
+            return
+        landed.add(key)
+        place = spot(dz, dy, k)
+        remote(
+            pool.at[place], pool.at[place], send_sem.at[0], recv_sem.at[place], across
+        ).wait_recv()
+
+    others = list(range(2, classes)) + [1]
+    mine = seq * head_count + head
+    for k in others:
+        copy = remote(
+            stage.at[k - 1], pool.at[mine], send_sem.at[len(pending)], recv_sem.at[mine],
+            {"seq": seq, "head": lane(k)},
+        )
+        copy.start()
+        pending.append(copy)
+    q_copies = []
+
+    def reach(flag):
+        if depth % 2:
+            return (depth - 1) // 2, (depth - 1) // 2
+        return (depth // 2, depth // 2 - 1) if flag else (depth // 2 - 1, depth // 2)
+
+    half = classes // 2
+    first_kind, second_kind = range(0, 2), range(2, classes)
+
+    def z_first_own(k):
+        arrive(0, 0, k)
+        push(0, 0, k, up)
+        push(0, 0, k, down)
+        push(0, 0, k, across)
+
+    def z_first_hop(k, t):
+        plus, minus = reach(k % 2 == 0)
+        if t <= plus:
+            arrive(-t, 0, k)
+            if t < plus:
+                push(-t, 0, k, up)
+            push(-t, 0, k, across)
+        if t <= minus:
+            arrive(t, 0, k)
+            if t < minus:
+                push(t, 0, k, down)
+            push(t, 0, k, across)
+
+    def y_first_own(k):
+        arrive(0, 0, k)
+        push(0, 0, k, across)
+        push(0, 0, k, up)
+        push(0, 0, k, down)
+
+    def y_first_partner(k):
+        arrive(0, 1, k)
+        push(0, 1, k, up)
+        push(0, 1, k, down)
+
+    def y_first_hop(k, t, dy):
+        plus, minus = reach(dy == 0)
+        if t <= plus:
+            arrive(-t, dy, k)
+            if t < plus:
+                push(-t, dy, k, up)
+        if t <= minus:
+            arrive(t, dy, k)
+            if t < minus:
+                push(t, dy, k, down)
+
+    def fold(dz, dy, kind):
+        ks = (0, 1) if kind == 0 else (2, 3)
+        for k in ks:
+            arrive(dz, dy, k)
+        low = (head // 2 + kind) % (head_count // 2) * 2
+        place = shard(dz, dy) * head_count + low
+
+        for hd in range(heads_dev):
+            cols = slice(hd * HEAD_DIM, (hd + 1) * HEAD_DIM)
+            query = q_all[:, :, cols].reshape(tokens, HEAD_DIM)
+            old_peak = peak_ref[pl.ds(hd, 1), :]
+            new_peak = old_peak
+            parts = []
+            for n in range(2):
+                block = place + n
+                gap = query_block - block
+                count = jnp.where((gap >= -1) & (gap <= 1), 1, 0)
+                for g in range(glob_count):
+                    count += jnp.where(glob_ref[g] == block, 1, 0)
+                for r in range(rand_count):
+                    row = listed[pl.ds(hd * rand_count + r, 1), :]
+                    count += jnp.where(row == block, 1, 0)
+                count = jnp.where(glob_row > 0, 1, count)
+                scores = lax.dot_general(
+                    pool[place + n, 0, :, cols], query, (((1,), (1,)), ((), ())),
+                    preferred_element_type=jnp.float32,
+                ) * (1.0 / math.sqrt(HEAD_DIM))
+                top = jnp.max(scores, axis=0, keepdims=True)
+                new_peak = jnp.maximum(new_peak, jnp.where(count > 0, top, MASKED))
+                parts.append((scores, count))
+            fade = jnp.exp(old_peak - new_peak)
+            total = total_ref[pl.ds(hd, 1), :] * fade
+            acc = acc_ref[hd] * fade
+            for n, (scores, count) in enumerate(parts):
+                powers = jnp.exp(scores - jnp.where(count > 0, new_peak, -MASKED))
+                powers = powers * count.astype(jnp.float32)
+                total = total + jnp.sum(powers, axis=0, keepdims=True)
+                acc = acc + lax.dot_general(
+                    pool[place + n, 1, :, cols], powers.astype(jnp.bfloat16),
+                    (((0,), (0,)), ((), ())), preferred_element_type=jnp.float32,
+                )
+            peak_ref[pl.ds(hd, 1), :] = new_peak
+            total_ref[pl.ds(hd, 1), :] = total
+            acc_ref[hd] = acc
+
+    z_first_own(0)
+    for k in others:
+        copy = remote(
+            q_stage.at[k - 1], q_all.at[head], q_send_sem.at[k - 1], q_recv_sem.at[head],
+            {"seq": seq, "head": lane(k)},
+        )
+        copy.start()
+        q_copies.append(copy)
+    z_first_own(1)
+    y_first_own(2)
+    z_first_hop(0, 1)
+    y_first_own(3)
+    z_first_hop(1, 1)
+    for k in range(1, classes):
+        remote(
+            q_stage.at[0], q_all.at[lane(k)], q_send_sem.at[0], q_recv_sem.at[lane(k)], across
+        ).wait_recv()
+    fold(0, 0, 0)
+    y_first_partner(2)
+    y_first_partner(3)
+    fold(0, 0, 1)
+    fold(0, 1, 0)
+    waiting = [(0, 1, 1)]
+    for t in range(1, depth // 2 + 1):
+        for k in (2, 3):
+            y_first_hop(k, t, 0)
+        for k in (0, 1) if t > 1 else ():
+            z_first_hop(k, t)
+        for item in waiting:
+            fold(*item)
+        for k in (2, 3):
+            y_first_hop(k, t, 1)
+        steps = (-t, t) if 2 * t < depth else (t,)
+        waiting = [(dz, 0, 0) for dz in steps]
+        waiting += [(dz, 0, 1) for dz in steps] + [(dz, 1, 1) for dz in steps]
+        waiting += [(dz, 1, 0) for dz in steps]
+    for item in waiting:
+        fold(*item)
+    for hd in range(heads_dev):
+        done = acc_ref[hd] / total_ref[pl.ds(hd, 1), :]
+        out_ref[:, hd * HEAD_DIM : (hd + 1) * HEAD_DIM] = done.T
+    for copy in pending + q_copies:
+        copy.wait_send()
+
+
+def gathered(queries, keys, values, random_blocks, global_blocks):
+    seq_count, head_count = lax.axis_size("seq"), lax.axis_size("head")
+    rows, width = queries.shape[0], queries.shape[1] // head_count
+    heads_dev = width // HEAD_DIM
+    tokens = rows * head_count
+    rand_count, glob_count = random_blocks.shape[2], global_blocks.shape[0]
+    dma = pltpu.SemaphoreType.DMA
+    return pl.pallas_call(
+        functools.partial(gathered_kernel, seq_count, head_count, rand_count, glob_count),
+        out_shape=jax.ShapeDtypeStruct((tokens, width), jnp.float32),
+        in_specs=[pl.BlockSpec(memory_space=pl.ANY)] * 3
+        + [pl.BlockSpec(memory_space=pltpu.SMEM)] * 2,
+        out_specs=pl.BlockSpec(memory_space=pltpu.VMEM),
+        scratch_shapes=[
+            pltpu.VMEM((seq_count * head_count, 2, rows, width), jnp.bfloat16),
+            pltpu.VMEM((head_count, rows, width), jnp.bfloat16),
+            pltpu.VMEM((head_count - 1, 2, rows, width), jnp.bfloat16),
+            pltpu.VMEM((head_count - 1, rows, width), jnp.bfloat16),
+            pltpu.VMEM((heads_dev * rand_count, tokens), jnp.int32),
+            pltpu.VMEM((heads_dev, tokens), jnp.float32),
+            pltpu.VMEM((heads_dev, tokens), jnp.float32),
+            pltpu.VMEM((heads_dev, HEAD_DIM, tokens), jnp.float32),
+            dma((3 * head_count,)),
+            dma((head_count + 5 * seq_count,)),
+            dma((seq_count * head_count,)),
+            dma((head_count - 1,)),
+            dma((head_count,)),
+        ],
+        compiler_params=pltpu.CompilerParams(
+            collective_id=0, has_side_effects=True, vmem_limit_bytes=40 * 2**20
+        ),
+    )(queries, keys, values, random_blocks, global_blocks)
+
+
+def shards(queries, keys, values, random_blocks, global_blocks):
+    seq_count, head_count = lax.axis_size("seq"), lax.axis_size("head")
+    pool_bytes = 4 * seq_count * queries.size
+    fits = pool_bytes <= GATHER_LIMIT and queries.shape[0] == BLK
+    if fits and head_count == 4 and seq_count % 2 == 0 and seq_count >= 6:
+        return gathered(queries, keys, values, random_blocks, global_blocks)
+    return exchanged(queries, keys, values, random_blocks, global_blocks)
+
+
 def solution(mesh):
     in_specs = (
         P(("seq", "head"), None),

time: 228 us -> 67.5 us (0.30); the launches traced: 225 us -> 67.3 us
  blocking collectives: 108 us -> 0 us
  Pallas kernels: 0 us -> 62.8 us
  local copies, waits for them, and re-layouts: 29.2 us -> 4.46 us
  starting transfers between devices: 23.7 us -> 0 us
  waiting for transfers between devices: 23.4 us -> 0 us
  other arithmetic: 20.7 us -> 0 us
  between operations: 13.9 us -> 0.01 us
  matrix products: 5.95 us -> 0 us
    pallas_call x0 -> x1, Pallas kernels: none -> 62.8 us  [gathered(): pl.pallas_call(functools.partial(gathered_kernel, seq_count, head_count,...]
    all_gather x2 -> x0, blocking collectives: 61.7 us -> none  [combined_all(): pieces = jax.tree.map(lambda part: lax.all_gather(part, axis), value)]
    psum x1 -> x0, blocking collectives: 46.4 us -> none  [shards(): glob_rows = lax.psum(picked, 'seq').astype(jnp.bfloat16)]
    all_to_all x5 -> x0, waiting for transfers between devices: 23.4 us -> none  [the longest x1 5.91 us: shards(): lax.all_to_all(queries, 'head', split_axis=1, concat_axis=0, tiled=True)]
    all_to_all x5 -> x0, starting transfers between devices: 19.8 us -> none  [the longest x1 5.48 us: shards(): lax.all_to_all(served, 'seq', split_axis=0, concat_axis=0, tiled=True)]
    add x17 -> x0, other arithmetic: 13.5 us -> none  [the longest x7 8.46 us: merge_parts(): former[2] * former_fade[..., None] + latter[2] * latter_fade[..., None]]
    gather x4 -> x0, local copies, waits for them, and re-layouts: 6.53 us -> none  [the longest x2 3.5 us: shards(): arrived_pairs.reshape((seq_count * capacity,) + tail)[slot_ids]]
    dot_general x8 -> x0, matrix products: 5.95 us -> none  [the longest x1 1.65 us: shards(): jnp.einsum('jqhd,jwkhd->jhqwk', query_four, key_win, preferred_element_ty...]
  transfers between devices with their start and end apart: 8 -> 0, of which waited for: 5 -> 0; matrix products, arithmetic and copies ran while one was open for 18% -> 0% of each run, Pallas kernels for 0% -> 0%
where the time goes in v1:
time: 67.5 us; the launch traced here: 67.3 us
  Pallas kernels  62.8 us (93%)
  local copies, waits for them, and re-layouts  4.46 us (7%)
    pallas_call x1, Pallas kernels, gathered(): pl.pallas_call(functools.partial(gathered_kernel, seq_count, head_count,...  62.8 us
    unnamed x10, local copies, waits for them, and re-layouts  4.46 us

profile of v1, /device:TPU:0, one launch (start us, length us, event | category | flops | bytes accessed | tf_op | source)
XLA Modules:
  0.0 67.3 jit_solution(10588871720542045381)
XLA Ops:
  0.0 0.0 copy-start.3
  0.0 0.8 %copy.6.rand_ref = s32[4,4,3]{2,1,0:T(4,128)S(1)} copy(s32[4,4,3]{1,0,2:T(4,128)} %param.8) | data formatting | bytes 384 | tf_op args[3]
  0.8 0.0 copy-done.3
  0.8 0.0 copy-start
  0.8 0.9 %copy-done = bf16[64,2048]{1,0:T(8,128)(2,1)S(1)} copy-done((bf16[64,2048]{1,0:T(8,128)(2,1)S(1)}, bf16[64,2048]{1,0:T(8,128)(2,1)}, u32[]{:S(2)}) %copy-start) | copy-done | bytes 262168
  1.8 0.0 copy-start.1
  1.8 0.9 %copy-done.1 = bf16[64,2048]{1,0:T(8,128)(2,1)S(1)} copy-done((bf16[64,2048]{1,0:T(8,128)(2,1)S(1)}, bf16[64,2048]{1,0:T(8,128)(2,1)}, u32[]{:S(2)}) %copy-start.1) | copy-done | bytes 262168
  2.7 0.0 copy-start.2
  2.7 0.9 %copy-done.2 = bf16[64,2048]{1,0:T(8,128)(2,1)S(1)} copy-done((bf16[64,2048]{1,0:T(8,128)(2,1)S(1)}, bf16[64,2048]{1,0:T(8,128)(2,1)}, u32[]{:S(2)}) %copy-start.2) | copy-done | bytes 262168
  3.7 62.8 %shard_map.55 = f32[256,512]{1,0:T(8,128)S(1)} custom-call(bf16[64,2048]{1,0:T(8,128)(2,1)S(1)} %copy-done, bf16[64,2048]{1,0:T(8,128)(2,1)S(1)} %copy-done.1, bf16[64,2048]{1,0:T(8,128)(2,1)S(1)} %copy-done.2, s32[4,4,3]{2,1,0:T(4,128)S(1)} %copy.6.rand_ref, s32[2]{0:T(128)S(1)} %copy-done.3), custom_call_target="tpu_custom_call" | custom-call | tf_op jit(solution)/shard_map/pallas_call | solution.py:453
  66.5 0.8 %copy.8 = f32[256,512]{1,0:T(8,128)} copy(f32[256,512]{1,0:T(8,128)S(1)} %shard_map.55) | data formatting | bytes 1048576
Async XLA Ops:
  0.0 0.8 %copy-start.3 = (s32[2]{0:T(128)S(1)}, s32[2]{0:T(128)}, u32[]{:S(2)}) copy-start(s32[2]{0:T(128)} %glob_ref.1) | copy-start | bytes 28
  0.8 1.0 %copy-start = (bf16[64,2048]{1,0:T(8,128)(2,1)S(1)}, bf16[64,2048]{1,0:T(8,128)(2,1)}, u32[]{:S(2)}) copy-start(bf16[64,2048]{1,0:T(8,128)(2,1)} %q_hbm.1) | copy-start | bytes 786436
  1.8 0.9 %copy-start.1 = (bf16[64,2048]{1,0:T(8,128)(2,1)S(1)}, bf16[64,2048]{1,0:T(8,128)(2,1)}, u32[]{:S(2)}) copy-start(bf16[64,2048]{1,0:T(8,128)(2,1)} %k_hbm.1) | copy-start | bytes 786436
  2.7 0.9 %copy-start.2 = (bf16[64,2048]{1,0:T(8,128)(2,1)S(1)}, bf16[64,2048]{1,0:T(8,128)(2,1)}, u32[]{:S(2)}) copy-start(bf16[64,2048]{1,0:T(8,128)(2,1)} %v_hbm.1) | copy-start | bytes 786436

commit v2 on v1

--- a/solution.py
+++ b/solution.py
@@ -192,8 +192,8 @@
 def gathered_kernel(
     seq_count, head_count, rand_count, glob_count,
     q_hbm, k_hbm, v_hbm, rand_ref, glob_ref, out_ref,
-    pool, q_all, stage, q_stage, listed, peak_ref, total_ref, acc_ref,
-    local_sem, send_sem, recv_sem, q_send_sem, q_recv_sem,
+    pool, rand_vmem, q_all, stage, q_stage, listed, peak_ref, total_ref, acc_ref,
+    local_sem, send_sem, recv_sem, q_recv_sem,
 ):
     seq = lax.axis_index("seq")
     head = lax.axis_index("head")
@@ -213,6 +213,8 @@
     def spot(dz, dy, k):
         return shard(dz, dy) * head_count + lane(k)
 
+    names_copy = pltpu.make_async_copy(rand_ref, rand_vmem, local_sem.at[3 * classes])
+    names_copy.start()
     loads = []
     for k in range(classes):
         cols = pl.ds(pl.multiple_of(lane(k) * width, 128), width)
@@ -224,20 +226,27 @@
         ):
             trio.append(pltpu.make_async_copy(source.at[:, cols], dest, local_sem.at[k * 3 + n]))
         loads.append(trio)
-    for n in range(3):
-        for trio in loads if n == 2 else ():
-            trio[n].start()
-        for trio in loads if n == 0 else ():
-            trio[0].start()
-            trio[1].start()
+    for trio in loads:
+        trio[0].start()
+        trio[1].start()
+    for trio in loads:
+        trio[2].start()
 
     barrier = pltpu.get_barrier_semaphore()
     friends = [{"seq": seq, "head": lane(k)} for k in range(1, classes)]
     friends.append({"seq": shard(0, 1), "head": head})
-    friends.append({"seq": shard(1, 0), "head": head})
-    friends.append({"seq": shard(-1, 0), "head": head})
+    up = {"seq": shard(1, 0), "head": head}
+    down = {"seq": shard(-1, 0), "head": head}
+    across = {"seq": shard(0, 1), "head": head}
+
+    def greet(friend):
+        pl.semaphore_signal(barrier, inc=1, device_id=friend, device_id_type=pl.DeviceIdType.MESH)
+
     for friend in friends:
-        pl.semaphore_signal(barrier, inc=1, device_id=friend, device_id_type=pl.DeviceIdType.MESH)
+        greet(friend)
+    pl.when(z < depth - 1)(lambda: greet(up))
+    pl.when(z > 0)(lambda: greet(down))
+    names_copy.wait()
 
     query_block = seq * (tokens // BLK) + lax.broadcasted_iota(jnp.int32, (1, tokens), 1) // BLK
     local_block = lax.broadcasted_iota(jnp.int32, (1, tokens), 1) // BLK
@@ -245,7 +254,7 @@
         for r in range(rand_count):
             names = jnp.zeros((1, tokens), jnp.int32)
             for b in range(tokens // BLK):
-                names = jnp.where(local_block == b, rand_ref[b, hd, r], names)
+                names = jnp.where(local_block == b, rand_vmem[b, pl.ds(hd, 1), pl.ds(r, 1)], names)
             listed[pl.ds(hd * rand_count + r, 1), :] = names
     is_glob = query_block == glob_ref[0]
     for g in range(1, glob_count):
@@ -260,10 +269,14 @@
         trio[1].wait()
     for trio in loads:
         trio[2].wait()
-    pl.semaphore_wait(barrier, len(friends))
+    line_friends = (z + depth - 1) // depth + (2 * depth - 2 - z) // depth
+    pl.semaphore_wait(barrier, len(friends) + line_friends)
 
     pending = []
-    landed = {(0, 0, 0)}
+    landed = {(0, 0, 0, 2)}
+    everywhere = z >= 0
+    cuts = [(2,)] * (classes - 1) + [(0, 1)]
+    y_first = {(classes - 1, 0)}
 
     def remote(source, dest, sender, receiver, device):
         return pltpu.make_async_remote_copy(
@@ -271,92 +284,87 @@
             device_id=device, device_id_type=pl.DeviceIdType.MESH,
         )
 
-    def push(dz, dy, k, device):
+    def view(ref, place, cut):
+        return ref.at[place] if cut == 2 else ref.at[place, cut]
+
+    def post(source, dest, receiver, device, when=everywhere):
+        sender = send_sem.at[len(pending)]
+        pl.when(when)(lambda: remote(source, dest, sender, receiver, device).start())
+        pending.append((source, dest, sender, receiver, device, when))
+
+    def push(dz, dy, k, cut, device, when=everywhere):
         place = spot(dz, dy, k)
-        copy = remote(
-            pool.at[place], pool.at[place], send_sem.at[len(pending)], recv_sem.at[place], device
-        )
-        copy.start()
-        pending.append(copy)
-
-    up = {"seq": shard(1, 0), "head": head}
-    down = {"seq": shard(-1, 0), "head": head}
-    across = {"seq": shard(0, 1), "head": head}
-
-    def arrive(dz, dy, k):
-        key = (dz % depth, dy % 2, k)
+        piece = view(pool, place, cut)
+        post(piece, piece, recv_sem.at[place, cut % 2], device, when)
+
+    def exists(dz):
+        return z >= -dz if dz < 0 else z + dz < depth
+
+    def arrive(dz, dy, k, cut, when=everywhere):
+        key = (dz, dy, k, cut)
         if key in landed:
             return
         landed.add(key)
         place = spot(dz, dy, k)
-        remote(
-            pool.at[place], pool.at[place], send_sem.at[0], recv_sem.at[place], across
-        ).wait_recv()
+        piece = view(pool, place, cut)
+        pl.when(when)(
+            lambda: remote(
+                piece, piece, send_sem.at[0], recv_sem.at[place, cut % 2], across
+            ).wait_recv()
+        )
 
     others = list(range(2, classes)) + [1]
     mine = seq * head_count + head
     for k in others:
-        copy = remote(
-            stage.at[k - 1], pool.at[mine], send_sem.at[len(pending)], recv_sem.at[mine],
-            {"seq": seq, "head": lane(k)},
-        )
-        copy.start()
-        pending.append(copy)
-    q_copies = []
-
-    def reach(flag):
-        if depth % 2:
-            return (depth - 1) // 2, (depth - 1) // 2
-        return (depth // 2, depth // 2 - 1) if flag else (depth // 2 - 1, depth // 2)
-
-    half = classes // 2
-    first_kind, second_kind = range(0, 2), range(2, classes)
-
-    def z_first_own(k):
-        arrive(0, 0, k)
-        push(0, 0, k, up)
-        push(0, 0, k, down)
-        push(0, 0, k, across)
-
-    def z_first_hop(k, t):
-        plus, minus = reach(k % 2 == 0)
-        if t <= plus:
-            arrive(-t, 0, k)
-            if t < plus:
-                push(-t, 0, k, up)
-            push(-t, 0, k, across)
-        if t <= minus:
-            arrive(t, 0, k)
-            if t < minus:
-                push(t, 0, k, down)
-            push(t, 0, k, across)
-
-    def y_first_own(k):
-        arrive(0, 0, k)
-        push(0, 0, k, across)
-        push(0, 0, k, up)
-        push(0, 0, k, down)
-
-    def y_first_partner(k):
-        arrive(0, 1, k)
-        push(0, 1, k, up)
-        push(0, 1, k, down)
-
-    def y_first_hop(k, t, dy):
-        plus, minus = reach(dy == 0)
-        if t <= plus:
-            arrive(-t, dy, k)
-            if t < plus:
-                push(-t, dy, k, up)
-        if t <= minus:
-            arrive(t, dy, k)
-            if t < minus:
-                push(t, dy, k, down)
+        for cut in cuts[k]:
+            post(
+                view(stage, k - 1, cut), view(pool, mine, cut), recv_sem.at[mine, cut % 2],
+                {"seq": seq, "head": lane(k)},
+            )
+
+    def own(k):
+        for cut in cuts[k]:
+            arrive(0, 0, k, cut)
+            push(0, 0, k, cut, across)
+            push(0, 0, k, cut, up, z < depth - 1)
+            push(0, 0, k, cut, down, z > 0)
+
+    def onward(dz, dy, k, cut, cross):
+        here = exists(dz)
+        arrive(dz, dy, k, cut, here)
+        if dz < 0 and -dz < depth - 1:
+            push(dz, dy, k, cut, up, here & (z < depth - 1))
+        if dz > 0 and dz < depth - 1:
+            push(dz, dy, k, cut, down, here & (z > 0))
+        if cross:
+            push(dz, dy, k, cut, across, here)
+
+    def hop(k, t):
+        for cut in cuts[k]:
+            early = (k, cut) in y_first
+            for dz in (-t, t):
+                onward(dz, 0, k, cut, not early)
+
+    def partner_hop(t):
+        for k, cut in sorted(y_first):
+            for dz in (-t, t):
+                onward(dz, 1, k, cut, False)
+
+    def partner():
+        for k, cut in sorted(y_first):
+            arrive(0, 1, k, cut)
+            push(0, 1, k, cut, up, z < depth - 1)
+            push(0, 1, k, cut, down, z > 0)
 
     def fold(dz, dy, kind):
         ks = (0, 1) if kind == 0 else (2, 3)
+        here = exists(dz)
         for k in ks:
-            arrive(dz, dy, k)
+            for cut in cuts[k]:
+                arrive(dz, dy, k, cut, here)
+        pl.when(here)(functools.partial(folded, dz, dy, kind))
+
+    def folded(dz, dy, kind):
         low = (head // 2 + kind) % (head_count // 2) * 2
         place = shard(dz, dy) * head_count + low
 
@@ -398,49 +406,42 @@
             total_ref[pl.ds(hd, 1), :] = total
             acc_ref[hd] = acc
 
-    z_first_own(0)
+    own(0)
     for k in others:
-        copy = remote(
-            q_stage.at[k - 1], q_all.at[head], q_send_sem.at[k - 1], q_recv_sem.at[head],
-            {"seq": seq, "head": lane(k)},
-        )
-        copy.start()
-        q_copies.append(copy)
-    z_first_own(1)
-    y_first_own(2)
-    z_first_hop(0, 1)
-    y_first_own(3)
-    z_first_hop(1, 1)
+        post(q_stage.at[k - 1], q_all.at[head], q_recv_sem.at[head], {"seq": seq, "head": lane(k)})
+    own(1)
+    own(2)
+    hop(0, 1)
+    own(3)
+    hop(1, 1)
+    partner()
     for k in range(1, classes):
         remote(
-            q_stage.at[0], q_all.at[lane(k)], q_send_sem.at[0], q_recv_sem.at[lane(k)], across
+            q_stage.at[0], q_all.at[lane(k)], send_sem.at[0], q_recv_sem.at[lane(k)], across
         ).wait_recv()
     fold(0, 0, 0)
-    y_first_partner(2)
-    y_first_partner(3)
+    hop(2, 1)
     fold(0, 0, 1)
+    hop(3, 1)
     fold(0, 1, 0)
+    partner_hop(1)
     waiting = [(0, 1, 1)]
-    for t in range(1, depth // 2 + 1):
-        for k in (2, 3):
-            y_first_hop(k, t, 0)
-        for k in (0, 1) if t > 1 else ():
-            z_first_hop(k, t)
-        for item in waiting:
-            fold(*item)
-        for k in (2, 3):
-            y_first_hop(k, t, 1)
-        steps = (-t, t) if 2 * t < depth else (t,)
-        waiting = [(dz, 0, 0) for dz in steps]
-        waiting += [(dz, 0, 1) for dz in steps] + [(dz, 1, 1) for dz in steps]
-        waiting += [(dz, 1, 0) for dz in steps]
+    for t in range(1, depth):
+        waiting += [(dz, dy, kind) for dy in (0, 1) for kind in (0, 1) for dz in (-t, t)]
+        if t + 1 < depth:
+            for k in range(classes):
+                hop(k, t + 1)
+                for item in waiting[:2]:
+                    fold(*item)
+                waiting = waiting[2:]
+            partner_hop(t + 1)
     for item in waiting:
         fold(*item)
     for hd in range(heads_dev):
         done = acc_ref[hd] / total_ref[pl.ds(hd, 1), :]
         out_ref[:, hd * HEAD_DIM : (hd + 1) * HEAD_DIM] = done.T
-    for copy in pending + q_copies:
-        copy.wait_send()
+    for *parts, when in pending:
+        pl.when(when)(lambda parts=parts: remote(*parts).wait_send())
 
 
 def gathered(queries, keys, values, random_blocks, global_blocks):
@@ -453,11 +454,12 @@
     return pl.pallas_call(
         functools.partial(gathered_kernel, seq_count, head_count, rand_count, glob_count),
         out_shape=jax.ShapeDtypeStruct((tokens, width), jnp.float32),
-        in_specs=[pl.BlockSpec(memory_space=pl.ANY)] * 3
-        + [pl.BlockSpec(memory_space=pltpu.SMEM)] * 2,
+        in_specs=[pl.BlockSpec(memory_space=pltpu.HBM)] * 4
+        + [pl.BlockSpec(memory_space=pltpu.SMEM)],
         out_specs=pl.BlockSpec(memory_space=pltpu.VMEM),
         scratch_shapes=[
             pltpu.VMEM((seq_count * head_count, 2, rows, width), jnp.bfloat16),
+            pltpu.VMEM(random_blocks.shape, jnp.int32),
             pltpu.VMEM((head_count, rows, width), jnp.bfloat16),
             pltpu.VMEM((head_count - 1, 2, rows, width), jnp.bfloat16),
             pltpu.VMEM((head_count - 1, rows, width), jnp.bfloat16),
@@ -465,10 +467,9 @@
             pltpu.VMEM((heads_dev, tokens), jnp.float32),
             pltpu.VMEM((heads_dev, tokens), jnp.float32),
             pltpu.VMEM((heads_dev, HEAD_DIM, tokens), jnp.float32),
-            dma((3 * head_count,)),
-            dma((head_count + 5 * seq_count,)),
-            dma((seq_count * head_count,)),
-            dma((head_count - 1,)),
+            dma((3 * head_count + 1,)),
+            dma((10 * seq_count + 24,)),
+            dma((seq_count * head_count, 2)),
             dma((head_count,)),
         ],
         compiler_params=pltpu.CompilerParams(

time: 67.5 us -> 54.6 us (0.81)
  Pallas kernels: 62.8 us -> 49.9 us
    pallas_call x1, Pallas kernels: 62.8 us -> 49.9 us  [gathered(): pl.pallas_call(functools.partial(gathered_kernel, seq_count, head_count,...]
where the time goes in v2:
time: 54.6 us; the launch traced here: 54.3 us
  Pallas kernels  49.9 us (91%)
  local copies, waits for them, and re-layouts  4.46 us (8%)
    pallas_call x1, Pallas kernels, gathered(): pl.pallas_call(functools.partial(gathered_kernel, seq_count, head_count,...  49.9 us
    unnamed x10, local copies, waits for them, and re-layouts  4.46 us

profile of v2, /device:TPU:0, one launch (start us, length us, event | category | flops | bytes accessed | tf_op | source)
XLA Modules:
  0.0 54.3 jit_solution(13145330650139805691)
XLA Ops:
  0.0 0.0 copy-start.3
  0.0 0.8 %copy.6.rand_ref = s32[4,4,3]{2,1,0:T(4,128)S(1)} copy(s32[4,4,3]{1,0,2:T(4,128)} %param.8) | data formatting | bytes 384 | tf_op args[3]
  0.8 0.0 copy-done.3
  0.8 0.0 copy-start
  0.8 0.9 %copy-done = bf16[64,2048]{1,0:T(8,128)(2,1)S(1)} copy-done((bf16[64,2048]{1,0:T(8,128)(2,1)S(1)}, bf16[64,2048]{1,0:T(8,128)(2,1)}, u32[]{:S(2)}) %copy-start) | copy-done | bytes 262168
  1.8 0.0 copy-start.1
  1.8 0.9 %copy-done.1 = bf16[64,2048]{1,0:T(8,128)(2,1)S(1)} copy-done((bf16[64,2048]{1,0:T(8,128)(2,1)S(1)}, bf16[64,2048]{1,0:T(8,128)(2,1)}, u32[]{:S(2)}) %copy-start.1) | copy-done | bytes 262168
  2.7 0.0 copy-start.2
  2.7 0.9 %copy-done.2 = bf16[64,2048]{1,0:T(8,128)(2,1)S(1)} copy-done((bf16[64,2048]{1,0:T(8,128)(2,1)S(1)}, bf16[64,2048]{1,0:T(8,128)(2,1)}, u32[]{:S(2)}) %copy-start.2) | copy-done | bytes 262168
  3.7 49.9 %shard_map.55 = f32[256,512]{1,0:T(8,128)S(1)} custom-call(bf16[64,2048]{1,0:T(8,128)(2,1)S(1)} %copy-done, bf16[64,2048]{1,0:T(8,128)(2,1)S(1)} %copy-done.1, bf16[64,2048]{1,0:T(8,128)(2,1)S(1)} %copy-done.2, s32[4,4,3]{2,1,0:T(4,128)S(1)} %copy.6.rand_ref, s32[2]{0:T(128)S(1)} %copy-done.3), custom_call_target="tpu_custom_call" | custom-call | tf_op jit(solution)/shard_map/pallas_call | solution.py:454
  53.5 0.8 %copy.8 = f32[256,512]{1,0:T(8,128)} copy(f32[256,512]{1,0:T(8,128)S(1)} %shard_map.55) | data formatting | bytes 1048576
Async XLA Ops:
  0.0 0.8 %copy-start.3 = (s32[2]{0:T(128)S(1)}, s32[2]{0:T(128)}, u32[]{:S(2)}) copy-start(s32[2]{0:T(128)} %glob_ref.1) | copy-start | bytes 28
  0.8 1.0 %copy-start = (bf16[64,2048]{1,0:T(8,128)(2,1)S(1)}, bf16[64,2048]{1,0:T(8,128)(2,1)}, u32[]{:S(2)}) copy-start(bf16[64,2048]{1,0:T(8,128)(2,1)} %q_hbm.1) | copy-start | bytes 786436
  1.8 0.9 %copy-start.1 = (bf16[64,2048]{1,0:T(8,128)(2,1)S(1)}, bf16[64,2048]{1,0:T(8,128)(2,1)}, u32[]{:S(2)}) copy-start(bf16[64,2048]{1,0:T(8,128)(2,1)} %k_hbm.1) | copy-start | bytes 786436
  2.7 0.9 %copy-start.2 = (bf16[64,2048]{1,0:T(8,128)(2,1)S(1)}, bf16[64,2048]{1,0:T(8,128)(2,1)}, u32[]{:S(2)}) copy-start(bf16[64,2048]{1,0:T(8,128)(2,1)} %v_hbm.1) | copy-start | bytes 786436

commit v3 on v2

--- a/solution.py
+++ b/solution.py
@@ -473,7 +473,7 @@
             dma((head_count,)),
         ],
         compiler_params=pltpu.CompilerParams(
-            collective_id=0, has_side_effects=True, vmem_limit_bytes=40 * 2**20
+            collective_id=0, has_side_effects=True
         ),
     )(queries, keys, values, random_blocks, global_blocks)
 

time: 54.6 us -> 54.2 us (level)
  local copies, waits for them, and re-layouts: 4.46 us -> 3.25 us
  Pallas kernels: 49.9 us -> 50.6 us
    unnamed x10 -> x2, local copies, waits for them, and re-layouts: 4.46 us -> 3.25 us
    pallas_call x1, Pallas kernels: 49.9 us -> 50.6 us  [gathered(): pl.pallas_call(functools.partial(gathered_kernel, seq_count, head_count,...]
where the time goes in v3:
time: 54.2 us; the launch traced here: 53.9 us
  Pallas kernels  50.6 us (93%)
  local copies, waits for them, and re-layouts  3.25 us (6%)
    pallas_call x1, Pallas kernels, gathered(): pl.pallas_call(functools.partial(gathered_kernel, seq_count, head_count,...  50.6 us
    unnamed x2, local copies, waits for them, and re-layouts  3.25 us

profile of v3, /device:TPU:0, one launch (start us, length us, event | category | flops | bytes accessed | tf_op | source)
XLA Modules:
  0.0 53.9 jit_solution(495309970804187614)
XLA Ops:
  0.0 1.4 %copy.6.rand_ref = s32[4,4,3]{2,1,0:T(4,128)} copy(s32[4,4,3]{1,0,2:T(4,128)} %param.8) | data formatting | bytes 384 | tf_op args[3]
  1.4 50.6 %shard_map.55 = f32[256,512]{1,0:T(8,128)} custom-call(bf16[64,2048]{1,0:T(8,128)(2,1)} %q_hbm.1, bf16[64,2048]{1,0:T(8,128)(2,1)} %k_hbm.1, bf16[64,2048]{1,0:T(8,128)(2,1)} %v_hbm.1, s32[4,4,3]{2,1,0:T(4,128)} %copy.6.rand_ref, s32[2]{0:T(128)} %glob_ref.1), custom_call_target="tpu_custom_call" | custom-call | tf_op jit(solution)/shard_map/pallas_call | solution.py:454
  52.0 1.9 %copy.8 = f32[256,512]{1,0:T(8,128)} copy(f32[256,512]{1,0:T(8,128)} %shard_map.55) | data formatting | bytes 1048576
